TPU v7x, 32 devices: a whole 2x2x4 slice. The times are simulated.
32 devices in a mesh: gx: 2 (over y), gy: 4 (over z), gz: 4 (over x, core).
Axes of the slice: x: 2, y: 2, z: 4, core: 2. Of those that a mesh axis runs over, the one named last changes fastest.
Arguments:
- density: float32 [64, 64, 512], P('gx', 'gy', 'gz'), may hold values from -8 to 8
Outputs:
- potential: float32 [64, 64, 512], P('gx', 'gy', 'gz')
All inputs are finite; a program needn't handle non-finite values.
Results may differ from a plain program's by a relative error of at most 0.00002.
Values sent between devices are 32-bit elements; how exact they have to be, the bound alone decides.
A program may use at most 128 MiB of HBM per device.

v0:
```python
import functools

import jax
import jax.numpy as jnp
from jax import lax
from jax.experimental import pallas as pl
from jax.experimental.pallas import tpu as pltpu
from jax.sharding import PartitionSpec as P

LEVELS = 7
CSWEEPS = 4
rsd_beta = 0.5
centre = 4.0 + 2.0 * (1.0 + rsd_beta)
along = 1.0 + rsd_beta
inverse = 1.0 / centre
F32 = jnp.float32
LANES = 128
AXES = ("gx", "gy", "gz")
STEPS_XY = [(dx, dy) for dx in (-1, 0, 1) for dy in (-1, 0, 1) if (dx, dy) != (0, 0)]


def up_to(value, unit):
    return -(-value // unit) * unit


class Split:
    def __init__(self, block, margins, counts):
        self.block, self.margins, self.counts = block, margins, counts
        self.planes = block[0] + 2 * margins[0]
        self.rows = up_to(block[1] + 2 * margins[1], 8)
        self.lanes = up_to(block[2] + 2 * margins[2], LANES)
        self.per = LANES // margins[2]
        self.packs = -(-self.planes // self.per)
        self.shape = (self.planes, self.rows, self.lanes)

    def scratch(self):
        land_x = (2, self.margins[0], self.block[1], LANES)
        land_y = (2, self.planes, self.margins[1], LANES)
        stage_y = (2, self.block[0], self.margins[1], LANES)
        packed = (2, self.packs, self.rows, LANES)
        one = [
            pltpu.VMEM(land_x, F32),
            pltpu.VMEM(land_x, F32),
            pltpu.VMEM(land_y, F32),
            pltpu.VMEM(stage_y, F32),
            pltpu.VMEM(packed, F32),
            pltpu.VMEM(packed, F32),
            pltpu.SemaphoreType.DMA((10,)),
            pltpu.SemaphoreType.DMA((10,)),
        ]
        own = [
            pltpu.VMEM(self.shape, F32),
            pltpu.VMEM((self.planes + 2,) + self.shape[1:], F32),
            pltpu.VMEM((2,) + self.shape[1:], jnp.int32),
        ]
        return own, one, list(one)


class Whole:
    def __init__(self, size):
        self.size = size
        self.rows = up_to(size[1], 8)
        self.lanes = up_to(size[2], LANES)
        self.shape = (size[0], self.rows, self.lanes)

    def scratch(self):
        return [
            pltpu.VMEM(self.shape, F32),
            pltpu.VMEM((self.shape[0] + 2,) + self.shape[1:], F32),
        ]


def iota(shape, dim):
    return lax.broadcasted_iota(jnp.int32, shape, dim)


def dot(a, b):
    return jnp.dot(a, b, precision=lax.Precision.HIGHEST, preferred_element_type=F32)


def local_of(index, length, margin, total):
    return jnp.where(index < total - margin, index, index - total)


def beside_sum(below, here, above, size, rows, lanes):
    down, up = pltpu.roll(here, 1, 0), pltpu.roll(here, rows - 1, 0)
    left, right = pltpu.roll(here, 1, 1), pltpu.roll(here, lanes - 1, 1)
    if size is not None:
        if size[1] == rows:
            row = iota(here.shape, 0)
            down = jnp.where(row == 0, 0.0, down)
            up = jnp.where(row == rows - 1, 0.0, up)
        if size[2] == lanes:
            lane = iota(here.shape, 1)
            left = jnp.where(lane == 0, 0.0, left)
            right = jnp.where(lane == lanes - 1, 0.0, right)
    return (below + above + (down + up)) + along * (left + right)


def chunk_of(planes, most):
    best = planes
    for number in range(2, most + 1, 2):
        if planes % number == 0:
            best = number
    return best if planes > most else planes


def for_planes(planes, most, body):
    chunk = chunk_of(planes, most)
    if chunk == planes:
        body(0, planes)
        return

    def step(number, carry):
        body(number * chunk, chunk)
        return carry

    lax.fori_loop(0, planes // chunk, step, 0)


def half(field, source, masks, colour, keep, size, shape, most):
    planes, rows, lanes = shape

    def body(start, count):
        old = [field[start + number] for number in range(count + 2)]
        for number in range(count):
            here = old[number + 1]
            total = beside_sum(old[number], here, old[number + 2], size, rows, lanes)
            update = (source[start + number] + total) * inverse
            chosen = masks((number + colour) % 2, keep(start + number))
            field[start + number + 1] = jnp.where(chosen, update, here)

    for_planes(planes, most, body)


def first_half(field, source, masks, keep, shape, most):
    planes, rows, lanes = shape
    field[0] = jnp.zeros((rows, lanes), F32)
    field[planes + 1] = jnp.zeros((rows, lanes), F32)

    def body(start, count):
        for number in range(count):
            chosen = masks(number % 2, keep(start + number))
            field[start + number + 1] = jnp.where(chosen, source[start + number] * inverse, 0.0)

    for_planes(planes, most, body)


def sweeps(field, source, masks, keep, size, shape, most, halves):
    for colour in halves:
        half(field, source, masks, colour, keep, size, shape, most)


def restricted(field, source, pairs, first, block, size, shape, most):
    planes, rows, lanes = shape
    height = pairs.shape[1]
    count_x, count_y, count_z = block
    top = min(height, up_to(count_y, 8))
    if height > top:
        pairs[0 : count_x // 2, top:height] = jnp.zeros((count_x // 2, height - top, LANES), F32)

    def body(start, count):
        old = [field[first + start + number] for number in range(count + 2)]
        parts = []
        for number in range(count):
            here = old[number + 1]
            total = beside_sum(old[number], here, old[number + 2], size, rows, lanes)
            rest = source[first + start + number] - centre * here + total
            parts.append(rest[:top, :LANES])
        half_start = start // 2 if isinstance(start, int) else lax.div(start, 2)
        for number in range(count // 2):
            both = parts[2 * number] + parts[2 * number + 1]
            if top > count_y:
                both = jnp.where(iota(both.shape, 0) < count_y, both, 0.0)
            pairs[half_start + number, 0:top] = both

    for_planes(count_x, most, body)
    number = count_x // 2
    even = pairs[0:number, pl.ds(0, height // 2, stride=2), :]
    odd = pairs[0:number, pl.ds(1, height // 2, stride=2), :]
    lane, column = iota((LANES, LANES), 0), iota((LANES, LANES), 1)
    down = jnp.where((lane // 2 == column) & (lane < count_z), 0.5, 0.0).astype(F32)
    flat = (even + odd).reshape(number * (height // 2), LANES)
    return dot(flat, down).reshape(number, height // 2, LANES)


def device(place, steps):
    return tuple(place[which] + steps[which] for which in range(3))


def exists(place, steps, counts):
    found = None
    for which in range(3):
        if steps[which] == 0:
            continue
        other = place[which] + steps[which]
        here = (other >= 0) & (other < counts[which])
        found = here if found is None else found & here
    return found


class Exchange:
    def __init__(self, level, place, array, offset, refs):
        self.level, self.place, self.array, self.offset = level, place, array, offset
        (self.stage_x, self.land_x, self.land_y, self.stage_y) = refs[:4]
        (self.stage_z, self.land_z, self.sent, self.got) = refs[4:]

    def xy(self, number):
        level = self.level
        dx, dy = STEPS_XY[number]
        margin, length = level.margins[0], level.block[0]
        place = {1: 0, 0: margin, -1: margin + length}[dx]
        count = length if dx == 0 else margin
        origin = length - margin if dx == 1 else 0
        if dy == 0:
            source = self.stage_x.at[(dx + 1) // 2]
            target = self.land_x.at[(dx + 1) // 2]
        else:
            source = self.stage_y.at[(dy + 1) // 2, pl.ds(origin, count)]
            target = self.land_y.at[(dy + 1) // 2, pl.ds(place, count)]
        return (dx, dy, 0), (place, count), pltpu.make_async_remote_copy(
            src_ref=source,
            dst_ref=target,
            send_sem=self.sent.at[number],
            recv_sem=self.got.at[number],
            device_id=device(self.place, (dx, dy, 0)),
            device_id_type=pl.DeviceIdType.MESH,
        )

    def start_xy(self):
        level, array = self.level, self.array
        low = self.offset + level.margins[0]
        length, rows, margin = level.block[0], level.block[1], level.margins
        self.stage_y[0] = array[low : low + length, 0 : margin[1], 0:LANES]
        self.stage_y[1] = array[low : low + length, rows - margin[1] : rows, 0:LANES]
        self.stage_x[0] = array[low : low + margin[0], 0:rows, 0:LANES]
        self.stage_x[1] = array[low + length - margin[0] : low + length, 0:rows, 0:LANES]
        for number in range(8):
            steps, _, copy = self.xy(number)

            @pl.when(exists(self.place, steps, level.counts))
            def _():
                copy.start()

    def finish_xy(self):
        level, array = self.level, self.array
        rows, margin = level.block[1], level.margins[1]
        for number in range(8):
            steps, (place, count), copy = self.xy(number)
            back = tuple(-step for step in steps)

            @pl.when(exists(self.place, back, level.counts))
            def _():
                copy.wait_recv()
                low = self.offset + place
                if steps[1] == 0:
                    array[low : low + count, 0:rows, 0:LANES] = self.land_x[(steps[0] + 1) // 2]
                else:
                    first = level.rows - margin if steps[1] == 1 else rows
                    side = (steps[1] + 1) // 2
                    array[low : low + count, first : first + margin, 0:LANES] = self.land_y[
                        side, place : place + count
                    ]

    def z(self, side):
        return pltpu.make_async_remote_copy(
            src_ref=self.stage_z.at[side],
            dst_ref=self.land_z.at[side],
            send_sem=self.sent.at[8 + side],
            recv_sem=self.got.at[8 + side],
            device_id=device(self.place, (0, 0, 2 * side - 1)),
            device_id_type=pl.DeviceIdType.MESH,
        )

    def start_z(self):
        level, array = self.level, self.array
        margin, length = level.margins[2], level.block[2]
        lane = iota((level.rows, LANES), 1)
        for side in range(2):
            first = length - margin if side == 1 else 0
            for pack in range(level.packs):
                total = jnp.zeros((level.rows, LANES), F32)
                for number in range(min(level.per, level.planes - pack * level.per)):
                    plane = array[self.offset + pack * level.per + number, :, 0:LANES]
                    moved = pltpu.roll(plane, (number * margin - first) % LANES, 1)
                    total = jnp.where(lane // margin == number, moved, total)
                self.stage_z[side, pack] = total
        for side in range(2):
            @pl.when(exists(self.place, (0, 0, 2 * side - 1), level.counts))
            def _():
                self.z(side).start()

    def finish_z(self):
        level, array = self.level, self.array
        margin, length = level.margins[2], level.block[2]
        base = level.lanes - LANES
        lane = iota((level.rows, LANES), 1)
        have = []
        for side in range(2):
            there = exists(self.place, (0, 0, 1 - 2 * side), level.counts)
            have.append(there)

            @pl.when(there)
            def _():
                self.z(side).wait_recv()

        above = length - base
        take_above = (lane >= above) & (lane < above + margin) & have[0]
        take_below = (lane >= LANES - margin) & have[1]
        for pack in range(level.packs):
            from_above, from_below = self.land_z[0, pack], self.land_z[1, pack]
            for number in range(min(level.per, level.planes - pack * level.per)):
                plane = self.offset + pack * level.per + number
                high = pltpu.roll(from_above, (above - number * margin) % LANES, 1)
                low = pltpu.roll(from_below, (LANES - margin - number * margin) % LANES, 1)
                value = array[plane, :, base : level.lanes]
                value = jnp.where(take_above, high, value)
                array[plane, :, base : level.lanes] = jnp.where(take_below, low, value)

    def drain(self):
        for number in range(8):
            steps, _, copy = self.xy(number)

            @pl.when(exists(self.place, steps, self.level.counts))
            def _():
                copy.wait_send()

        for side in range(2):
            @pl.when(exists(self.place, (0, 0, 2 * side - 1), self.level.counts))
            def _():
                self.z(side).wait_send()


def solve_whole(levels, refs, pairs, number):
    level = levels[number]
    source, field = refs[number]
    planes, rows, lanes = level.shape
    row, lane = iota((rows, lanes), 0), iota((rows, lanes), 1)
    inside = (row < level.size[1]) & (lane < level.size[2])
    choices = [inside & ((row + lane) % 2 == colour) for colour in range(2)]

    def masks(which, keep):
        return choices[which]

    def keep(plane):
        return None

    first_half(field, source, masks, keep, level.shape, 8)
    if number == len(levels) - 1:
        sweeps(field, source, masks, keep, level.size, level.shape, 8, (1,) + (0, 1) * (CSWEEPS - 1))
        return
    sweeps(field, source, masks, keep, level.size, level.shape, 8, (1, 0, 1))
    coarse = levels[number + 1]
    height = 2 * coarse.rows
    hold = pairs.at[:, 0:height]
    below = restricted(field, source, hold, 0, level.size, level.size, level.shape, 8)
    refs[number + 1][0][...] = below
    solve_whole(levels, refs, pairs, number + 1)
    count = coarse.shape[0]
    solved = refs[number + 1][1][1 : 1 + count]
    column, target = iota((LANES, LANES), 0), iota((LANES, LANES), 1)
    spread = jnp.where(target // 2 == column, 1.0, 0.0).astype(F32)
    flat = dot(solved.reshape(count * coarse.rows, LANES), spread)
    flat = flat.reshape(count, coarse.rows, LANES)
    pairs[0:count, pl.ds(0, coarse.rows, stride=2), :] = flat
    pairs[0:count, pl.ds(1, coarse.rows, stride=2), :] = flat
    for plane in range(planes):
        field[plane + 1] = field[plane + 1] + pairs[plane // 2, 0:rows]
    sweeps(field, source, masks, keep, level.size, level.shape, 8, (0, 1, 0, 1))


def kernel(splits, levels, counts, density, potential, *refs):
    place = tuple(lax.axis_index(axis) for axis in AXES)
    total = counts[0] * counts[1] * counts[2]
    me = (place[0] * counts[1] + place[1]) * counts[2] + place[2]
    refs = list(refs)

    def take(number):
        taken = refs[:number]
        del refs[:number]
        return taken

    parts = []
    for level in splits:
        source, field, mask = take(3)
        of_source = Exchange(level, place, source, 0, take(8))
        of_field = Exchange(level, place, field, 1, take(8))
        parts.append((source, field, mask, of_source, of_field))
    whole_refs = [take(2) for _ in levels]
    pairs, spreads, own, slots, sent, got = take(6)

    def peer(number):
        other = lax.rem(me + number, total)
        inner = counts[1] * counts[2]
        return (lax.div(other, inner), lax.rem(lax.div(other, counts[2]), counts[1]), lax.rem(other, counts[2])), other

    barrier = pltpu.get_barrier_semaphore()

    def greet(number, carry):
        pl.semaphore_signal(
            barrier, inc=1, device_id=peer(number)[0], device_id_type=pl.DeviceIdType.MESH
        )
        return carry

    lax.fori_loop(1, total, greet, 0)

    for level, (source, field, mask, of_source, of_field) in zip(splits, parts):
        source[...] = jnp.zeros(level.shape, F32)
        plane = (level.rows, level.lanes)
        inside = None
        for dim in (1, 2):
            index = iota(plane, dim - 1)
            size = level.rows if dim == 1 else level.lanes
            margin, length = level.margins[dim], level.block[dim]
            used = (index < length + margin) | (index >= size - margin)
            spot = local_of(index, length, margin, size) + place[dim] * length
            used = used & (spot >= 0) & (spot < length * counts[dim])
            inside = used if inside is None else inside & used
        parity = (iota(plane, 0) + iota(plane, 1)) % 2
        for colour in range(2):
            mask[colour] = jnp.where(inside & (parity == colour), 1, 0)
    first = splits[0]
    parts[0][0][
        first.margins[0] : first.margins[0] + first.block[0], 0 : first.block[1], 0 : first.block[2]
    ] = density[...]
    pl.semaphore_wait(barrier, total - 1)

    def keep_of(level):
        def keep(plane):
            spot = place[0] * level.block[0] + plane - level.margins[0]
            return jnp.where((spot >= 0) & (spot < level.block[0] * counts[0]), 1, 0)

        return keep

    def masks_of(mask):
        def masks(which, keep):
            return (mask[which] & keep) != 0

        return masks

    def descend(number):
        level = splits[number]
        source, field, mask, of_source, _ = parts[number]
        masks, keep = masks_of(mask), keep_of(level)
        first_half(field, source, masks, keep, level.shape, 8)
        sweeps(field, source, masks, keep, None, level.shape, 8, (1, 0, 1))
        height = 2 * up_to(level.block[1] // 2, 8)
        return restricted(
            field, source, pairs.at[:, 0:height], level.margins[0], level.block, None, level.shape, 8
        )

    def ascend(number, coarse_plane, rows_to, lanes_to, reach):
        level = splits[number]
        source, field, mask, _, _ = parts[number]
        masks, keep = masks_of(mask), keep_of(level)
        for spot in range(reach):
            spreads[spot] = dot(rows_to, coarse_plane(spot))
        flat = dot(spreads[0:reach].reshape(reach * level.rows, LANES), lanes_to)
        flat = flat.reshape(reach, level.rows, level.lanes)
        for plane in range(level.planes):
            added = jnp.where(keep(plane) != 0, flat[plane // 2], 0.0)
            field[plane + 1] = field[plane + 1] + added
        sweeps(field, source, masks, keep, None, level.shape, 8, (0, 1, 0, 1))

    top, next_ = splits
    top_parts, next_parts = parts
    top_parts[3].start_xy()
    top_parts[3].finish_xy()
    top_parts[3].start_z()
    top_parts[3].finish_z()
    below = descend(0)
    next_parts[0][
        next_.margins[0] : next_.margins[0] + next_.block[0], 0 : next_.block[1], 0:LANES
    ] = below
    next_parts[3].start_xy()
    top_parts[4].start_xy()
    next_parts[3].finish_xy()
    next_parts[3].start_z()
    next_parts[3].finish_z()
    below = descend(1)

    length = tuple(size // 2 for size in next_.block)
    per = LANES // length[2]
    packed = jnp.zeros((8, LANES), F32)
    for plane in range(length[0]):
        moved = below[plane]
        if plane // per:
            moved = pltpu.roll(moved, length[1] * (plane // per), 0)
        if plane % per:
            moved = pltpu.roll(moved, length[2] * (plane % per), 1)
        packed = packed + moved
    own[...] = packed
    slots[me] = packed

    def send(number):
        target, other = peer(number)
        return pltpu.make_async_remote_copy(
            src_ref=own,
            dst_ref=slots.at[me],
            send_sem=sent.at[other],
            recv_sem=got.at[me],
            device_id=target,
            device_id_type=pl.DeviceIdType.MESH,
        )

    def start_send(number, carry):
        send(number).start()
        return carry

    lax.fori_loop(1, total, start_send, 0)
    next_parts[4].start_xy()
    top_parts[4].finish_xy()
    top_parts[4].start_z()
    next_parts[4].finish_xy()
    next_parts[4].start_z()

    def finish_send(number, carry):
        target, other = peer(number)
        copy = pltpu.make_async_remote_copy(
            src_ref=own,
            dst_ref=slots.at[other],
            send_sem=sent.at[other],
            recv_sem=got.at[other],
            device_id=target,
            device_id_type=pl.DeviceIdType.MESH,
        )
        copy.wait_recv()
        copy.wait_send()
        return carry

    lax.fori_loop(1, total, finish_send, 0)

    coarse_source, coarse_field = whole_refs[0]
    lane = iota((8, LANES), 1)

    def place_x(which, carry):
        for second in range(counts[1]):
            base = (which * counts[1] + second) * counts[2]
            tiles = [slots[base + third] for third in range(counts[2])]
            for spot in range(per):
                value = jnp.zeros((8, LANES), F32)
                for third in range(counts[2]):
                    shift = (length[2] * (third - spot)) % LANES
                    moved = pltpu.roll(tiles[third], shift, 1) if shift else tiles[third]
                    value = jnp.where(lane // length[2] == third, moved, value)
                for group in range(8 // length[1]):
                    plane = which * length[0] + group * per + spot
                    coarse_source[plane, second * length[1] : (second + 1) * length[1], :] = value[
                        group * length[1] : (group + 1) * length[1]
                    ]
        return carry

    lax.fori_loop(0, counts[0], place_x, 0)
    solve_whole(levels, whole_refs, pairs, 0)

    def one_hot(shape, dim, fine, fine_length, fine_margin, origin, wrap):
        index = iota(shape, dim)
        spot = local_of(index, fine_length, fine_margin, fine)
        cell = jnp.where(spot >= 0, lax.div(spot, 2), -lax.div(1 - spot, 2)) + origin
        if wrap is not None:
            cell = jnp.where(cell < 0, cell + wrap, cell)
        used = (index < fine_length + fine_margin) | (index >= fine - fine_margin)
        return jnp.where((iota(shape, 1 - dim) == cell) & used, 1.0, 0.0).astype(F32)

    coarse = levels[0]
    rows_to = one_hot(
        (next_.rows, coarse.rows), 0, next_.rows, next_.block[1], next_.margins[1],
        place[1] * length[1], None,
    )
    lanes_to = one_hot(
        (LANES, next_.lanes), 1, next_.lanes, next_.block[2], next_.margins[2],
        place[2] * length[2], None,
    )
    reach = next_.planes // 2

    def plane_of_whole(spot):
        plane = place[0] * length[0] + spot - next_.margins[0] // 2
        return coarse_field[1 + jnp.clip(plane, 0, coarse.shape[0] - 1)]

    next_parts[4].finish_z()
    ascend(1, plane_of_whole, rows_to, lanes_to, reach)

    rows_to = one_hot(
        (top.rows, next_.rows), 0, top.rows, top.block[1], top.margins[1], 0, next_.rows
    )
    lanes_to = one_hot(
        (LANES, top.lanes), 1, top.lanes, top.block[2], top.margins[2], 0, next_.lanes
    )
    shift = next_.margins[0] - top.margins[0] // 2
    top_parts[4].finish_z()
    ascend(0, lambda spot: next_parts[1][1 + spot + shift], rows_to, lanes_to, top.planes // 2)
    potential[...] = top_parts[1][
        1 + top.margins[0] : 1 + top.margins[0] + top.block[0], 0 : top.block[1], 0 : top.block[2]
    ]
    for part in parts:
        part[3].drain()
        part[4].drain()


def flat_scratch(entries):
    out = []
    for entry in entries:
        out.extend(flat_scratch(entry) if isinstance(entry, (list, tuple)) else [entry])
    return out


def on_device(counts, density):
    block = density.shape
    half_block = tuple(size // 2 for size in block)
    splits = [
        Split(block, (4, 4, 4), counts),
        Split(half_block, (6, 8, 8), counts),
    ]
    size = tuple(block[which] * counts[which] // 4 for which in range(3))
    levels = []
    for number in range(2, LEVELS):
        levels.append(Whole(size))
        size = tuple(max(part // 2, 1) for part in size)
    total = counts[0] * counts[1] * counts[2]
    pair_planes = max(block[0] // 2, levels[0].shape[0])
    pair_rows = max(block[1], levels[0].rows, 16)
    scratch = [level.scratch() for level in splits] + [level.scratch() for level in levels]
    scratch = flat_scratch(scratch) + [
        pltpu.VMEM((pair_planes, pair_rows, LANES), F32),
        pltpu.VMEM((max(level.planes // 2 for level in splits), splits[0].rows, LANES), F32),
        pltpu.VMEM((8, LANES), F32),
        pltpu.VMEM((total, 8, LANES), F32),
        pltpu.SemaphoreType.DMA((total,)),
        pltpu.SemaphoreType.DMA((total,)),
    ]
    return pl.pallas_call(
        functools.partial(kernel, splits, levels, counts),
        out_shape=jax.ShapeDtypeStruct(block, F32),
        in_specs=[pl.BlockSpec(memory_space=pltpu.VMEM)],
        out_specs=pl.BlockSpec(memory_space=pltpu.VMEM),
        scratch_shapes=scratch,
        compiler_params=pltpu.CompilerParams(
            collective_id=0, has_side_effects=True, vmem_limit_bytes=48 * 1024 * 1024
        ),
    )(density)


def solution(mesh):
    counts = tuple(mesh.shape[axis] for axis in AXES)
    return jax.shard_map(
        functools.partial(on_device, counts),
        mesh=mesh,
        in_specs=(P("gx", "gy", "gz"),),
        out_specs=P("gx", "gy", "gz"),
        check_vma=False,
    )
```

profile of v0, /device:TPU:1, one launch (start us, length us, event | category | flops | bytes accessed | tf_op | source)
XLA Modules:
  0.0 48.3 jit_solution(12636212534153126127)
XLA Ops:
  0.0 0.0 copy-start
  0.0 0.9 %copy-done = f32[32,16,128]{2,1,0:T(8,128)S(1)} copy-done((f32[32,16,128]{2,1,0:T(8,128)S(1)}, f32[32,16,128]{2,1,0:T(8,128)}, u32[]{:S(2)}) %copy-start) | copy-done | bytes 262168
  1.0 46.6 %shard_map.17 = f32[32,16,128]{2,1,0:T(8,128)S(1)} custom-call(f32[32,16,128]{2,1,0:T(8,128)S(1)} %copy-done), custom_call_target="tpu_custom_call" | custom-call | tf_op jit(solution)/shard_map/pallas_call | solution.py:631
  47.6 0.7 %copy.3 = f32[32,16,128]{2,1,0:T(8,128)} copy(f32[32,16,128]{2,1,0:T(8,128)S(1)} %shard_map.17) | data formatting | bytes 524288
Async XLA Ops:
  0.0 0.9 %copy-start = (f32[32,16,128]{2,1,0:T(8,128)S(1)}, f32[32,16,128]{2,1,0:T(8,128)}, u32[]{:S(2)}) copy-start(f32[32,16,128]{2,1,0:T(8,128)} %density.1) | copy-start | bytes 786436
where the time goes:
time: 48.5 us; the launch traced here: 48.3 us
  Pallas kernels  46.6 us (96%)
  local copies, waits for them, and re-layouts  1.65 us (3%)
    pallas_call x1, Pallas kernels, on_device(): pl.pallas_call(functools.partial(kernel, splits, levels, counts), out_sha...  46.6 us
    unnamed x3, local copies, waits for them, and re-layouts  1.65 us

commit v1 on v0

--- a/solution.py
+++ b/solution.py
@@ -74,8 +74,21 @@
     return lax.broadcasted_iota(jnp.int32, shape, dim)
 
 
-def dot(a, b):
-    return jnp.dot(a, b, precision=lax.Precision.HIGHEST, preferred_element_type=F32)
+def pieces(value):
+    high = value.astype(jnp.bfloat16)
+    rest = value - high.astype(F32)
+    middle = rest.astype(jnp.bfloat16)
+    return high, middle, (rest - middle.astype(F32)).astype(jnp.bfloat16)
+
+
+def dot(value, chosen):
+    chosen = chosen.astype(jnp.bfloat16)
+    parts = [jnp.dot(part, chosen, preferred_element_type=F32) for part in pieces(value)]
+    return parts[0] + (parts[1] + parts[2])
+
+
+def dot_rows(chosen, value):
+    return jnp.dot(chosen, value, precision=lax.Precision.HIGHEST, preferred_element_type=F32)
 
 
 def local_of(index, length, margin, total):
@@ -98,39 +111,38 @@
 
 
 def chunk_of(planes, most):
-    best = planes
-    for number in range(2, most + 1, 2):
-        if planes % number == 0:
-            best = number
-    return best if planes > most else planes
-
-
-def for_planes(planes, most, body):
+    if planes <= most:
+        return planes
+    return max([number for number in range(2, most + 1, 2) if planes % number == 0])
+
+
+def for_planes(first, planes, most, body):
     chunk = chunk_of(planes, most)
     if chunk == planes:
-        body(0, planes)
+        body(first, planes)
         return
 
     def step(number, carry):
-        body(number * chunk, chunk)
+        body(first + number * chunk, chunk)
         return carry
 
     lax.fori_loop(0, planes // chunk, step, 0)
 
 
-def half(field, source, masks, colour, keep, size, shape, most):
+def half(field, source, masks, colour, keep, size, shape, most, skip=0):
     planes, rows, lanes = shape
 
     def body(start, count):
-        old = [field[start + number] for number in range(count + 2)]
+        before, here = field[start], field[start + 1]
         for number in range(count):
-            here = old[number + 1]
-            total = beside_sum(old[number], here, old[number + 2], size, rows, lanes)
+            after = field[start + number + 2]
+            total = beside_sum(before, here, after, size, rows, lanes)
             update = (source[start + number] + total) * inverse
-            chosen = masks((number + colour) % 2, keep(start + number))
+            chosen = masks((number + skip + colour) % 2, keep(start + number))
             field[start + number + 1] = jnp.where(chosen, update, here)
-
-    for_planes(planes, most, body)
+            before, here = here, after
+
+    for_planes(skip, planes - 2 * skip, most, body)
 
 
 def first_half(field, source, masks, keep, shape, most):
@@ -143,12 +155,13 @@
             chosen = masks(number % 2, keep(start + number))
             field[start + number + 1] = jnp.where(chosen, source[start + number] * inverse, 0.0)
 
-    for_planes(planes, most, body)
-
-
-def sweeps(field, source, masks, keep, size, shape, most, halves):
-    for colour in halves:
-        half(field, source, masks, colour, keep, size, shape, most)
+    for_planes(0, planes, most, body)
+
+
+def sweeps(field, source, masks, keep, size, shape, most, halves, skips=None):
+    for number, colour in enumerate(halves):
+        skip = 0 if skips is None else skips[number]
+        half(field, source, masks, colour, keep, size, shape, most, skip)
 
 
 def restricted(field, source, pairs, first, block, size, shape, most):
@@ -174,7 +187,7 @@
                 both = jnp.where(iota(both.shape, 0) < count_y, both, 0.0)
             pairs[half_start + number, 0:top] = both
 
-    for_planes(count_x, most, body)
+    for_planes(0, count_x, most, body)
     number = count_x // 2
     even = pairs[0:number, pl.ds(0, height // 2, stride=2), :]
     odd = pairs[0:number, pl.ds(1, height // 2, stride=2), :]
@@ -345,15 +358,15 @@
     def keep(plane):
         return None
 
-    first_half(field, source, masks, keep, level.shape, 8)
+    first_half(field, source, masks, keep, level.shape, 16)
     if number == len(levels) - 1:
-        sweeps(field, source, masks, keep, level.size, level.shape, 8, (1,) + (0, 1) * (CSWEEPS - 1))
+        sweeps(field, source, masks, keep, level.size, level.shape, 16, (1,) + (0, 1) * (CSWEEPS - 1))
         return
-    sweeps(field, source, masks, keep, level.size, level.shape, 8, (1, 0, 1))
+    sweeps(field, source, masks, keep, level.size, level.shape, 16, (1, 0, 1))
     coarse = levels[number + 1]
     height = 2 * coarse.rows
     hold = pairs.at[:, 0:height]
-    below = restricted(field, source, hold, 0, level.size, level.size, level.shape, 8)
+    below = restricted(field, source, hold, 0, level.size, level.size, level.shape, 16)
     refs[number + 1][0][...] = below
     solve_whole(levels, refs, pairs, number + 1)
     count = coarse.shape[0]
@@ -366,7 +379,7 @@
     pairs[0:count, pl.ds(1, coarse.rows, stride=2), :] = flat
     for plane in range(planes):
         field[plane + 1] = field[plane + 1] + pairs[plane // 2, 0:rows]
-    sweeps(field, source, masks, keep, level.size, level.shape, 8, (0, 1, 0, 1))
+    sweeps(field, source, masks, keep, level.size, level.shape, 16, (0, 1, 0, 1))
 
 
 def kernel(splits, levels, counts, density, potential, *refs):
@@ -404,8 +417,15 @@
 
     lax.fori_loop(1, total, greet, 0)
 
+    first = splits[0]
+    parts[0][0][
+        first.margins[0] : first.margins[0] + first.block[0], 0 : first.block[1], 0 : first.block[2]
+    ] = density[...]
+    pl.semaphore_wait(barrier, total - 1)
+
+    parts[0][3].start_xy()
+
     for level, (source, field, mask, of_source, of_field) in zip(splits, parts):
-        source[...] = jnp.zeros(level.shape, F32)
         plane = (level.rows, level.lanes)
         inside = None
         for dim in (1, 2):
@@ -419,11 +439,6 @@
         parity = (iota(plane, 0) + iota(plane, 1)) % 2
         for colour in range(2):
             mask[colour] = jnp.where(inside & (parity == colour), 1, 0)
-    first = splits[0]
-    parts[0][0][
-        first.margins[0] : first.margins[0] + first.block[0], 0 : first.block[1], 0 : first.block[2]
-    ] = density[...]
-    pl.semaphore_wait(barrier, total - 1)
 
     def keep_of(level):
         def keep(plane):
@@ -438,15 +453,24 @@
 
         return masks
 
+    edges = [level.margins[0] for level in splits]
+    before = [tuple(edge - reach for reach in (3, 2, 1)) for edge in edges]
+    final = (0, splits[0].margins[0] // 2)
+    after = [
+        tuple(edge - reach - last for reach in (3, 2, 1, 0)) for edge, last in zip(edges, final)
+    ]
+    before[0] = tuple(skip - skip % 2 for skip in before[0])
+    after[0] = tuple(skip - skip % 2 for skip in after[0])
+
     def descend(number):
         level = splits[number]
         source, field, mask, of_source, _ = parts[number]
         masks, keep = masks_of(mask), keep_of(level)
-        first_half(field, source, masks, keep, level.shape, 8)
-        sweeps(field, source, masks, keep, None, level.shape, 8, (1, 0, 1))
+        first_half(field, source, masks, keep, level.shape, 20)
+        sweeps(field, source, masks, keep, None, level.shape, 26, (1, 0, 1), before[number])
         height = 2 * up_to(level.block[1] // 2, 8)
         return restricted(
-            field, source, pairs.at[:, 0:height], level.margins[0], level.block, None, level.shape, 8
+            field, source, pairs.at[:, 0:height], level.margins[0], level.block, None, level.shape, 16
         )
 
     def ascend(number, coarse_plane, rows_to, lanes_to, reach):
@@ -454,17 +478,16 @@
         source, field, mask, _, _ = parts[number]
         masks, keep = masks_of(mask), keep_of(level)
         for spot in range(reach):
-            spreads[spot] = dot(rows_to, coarse_plane(spot))
+            spreads[spot] = dot_rows(rows_to, coarse_plane(spot))
         flat = dot(spreads[0:reach].reshape(reach * level.rows, LANES), lanes_to)
         flat = flat.reshape(reach, level.rows, level.lanes)
         for plane in range(level.planes):
             added = jnp.where(keep(plane) != 0, flat[plane // 2], 0.0)
             field[plane + 1] = field[plane + 1] + added
-        sweeps(field, source, masks, keep, None, level.shape, 8, (0, 1, 0, 1))
+        sweeps(field, source, masks, keep, None, level.shape, 26, (0, 1, 0, 1), after[number])
 
     top, next_ = splits
     top_parts, next_parts = parts
-    top_parts[3].start_xy()
     top_parts[3].finish_xy()
     top_parts[3].start_z()
     top_parts[3].finish_z()

time: 48.5 us -> 40.7 us (0.84)
  Pallas kernels: 46.6 us -> 38.9 us
    pallas_call x1, Pallas kernels: 46.6 us -> 38.9 us  [on_device(): pl.pallas_call(functools.partial(kernel, splits, levels, counts), out_sha...]
where the time goes in v1:
time: 40.7 us; the launch traced here: 40.5 us
  Pallas kernels  38.9 us (96%)
  local copies, waits for them, and re-layouts  1.65 us (4%)
    pallas_call x1, Pallas kernels, on_device(): pl.pallas_call(functools.partial(kernel, splits, levels, counts), out_sha...  38.9 us
    unnamed x3, local copies, waits for them, and re-layouts  1.65 us

profile of v1, /device:TPU:1, one launch (start us, length us, event | category | flops | bytes accessed | tf_op | source)
XLA Modules:
  0.0 40.5 jit_solution(3626255930020597299)
XLA Ops:
  0.0 0.0 copy-start
  0.0 0.9 %copy-done = f32[32,16,128]{2,1,0:T(8,128)S(1)} copy-done((f32[32,16,128]{2,1,0:T(8,128)S(1)}, f32[32,16,128]{2,1,0:T(8,128)}, u32[]{:S(2)}) %copy-start) | copy-done | bytes 262168
  1.0 38.9 %shard_map.17 = f32[32,16,128]{2,1,0:T(8,128)S(1)} custom-call(f32[32,16,128]{2,1,0:T(8,128)S(1)} %copy-done), custom_call_target="tpu_custom_call" | custom-call | tf_op jit(solution)/shard_map/pallas_call | solution.py:654
  39.8 0.7 %copy.3 = f32[32,16,128]{2,1,0:T(8,128)} copy(f32[32,16,128]{2,1,0:T(8,128)S(1)} %shard_map.17) | data formatting | bytes 524288
Async XLA Ops:
  0.0 0.9 %copy-start = (f32[32,16,128]{2,1,0:T(8,128)S(1)}, f32[32,16,128]{2,1,0:T(8,128)}, u32[]{:S(2)}) copy-start(f32[32,16,128]{2,1,0:T(8,128)} %density.1) | copy-start | bytes 786436
